TPU v7x, 128 devices: a whole 4x4x4 slice. The times are simulated.
128 devices in a mesh: step: 2 (over core), tile: 64 (over z, y, x).
Axes of the slice: x: 4, y: 4, z: 4, core: 2. Of those that a mesh axis runs over, the one named last changes fastest.
Arguments:
- latents: float32 [2, 8192, 3072], P('step', 'tile'), may hold values from -6 to 6
- start: float32 [8192, 3072], P('tile'), may hold values from -6 to 6
- cached_velocity: float32 [2, 8192, 3072], P('step', 'tile'), may hold values from -4 to 4
- shift: float32 [2, 3072], P('step'), may hold values from -3 to 3
- scale: float32 [2, 3072], P('step'), may hold values from -3 to 3
- gate: float32 [2, 3072], P('step'), may hold values from -10 to 10
- step_sizes: float32 [2], P('step'), may hold values from 0.1 to 0.5
- converged: int32 [2, 64], P(None, 'tile'), may hold values from 0 to 1, as said below
- neighbours: int32 [64, 4], P('tile'), may hold values from 0 to 1, as said below
- w_qkv: bfloat16 [3, 3072, 2048], P(None, None, 'step'), may hold values from -0.109375 to 0.109375
- q_gain: float32 [128], replicated, may hold values from 0.1 to 1.9
- k_gain: float32 [128], replicated, may hold values from 0.1 to 1.9
- w_out: bfloat16 [2048, 3072], P('step', 'tile'), may hold values from -0.5 to 0.5
Outputs:
- updated: float32 [2, 8192, 3072], P('step', 'tile')
- velocity: float32 [2, 8192, 3072], P('step', 'tile')
Inputs may be any that keep to these rules, and one draw needn't show every extreme that they name: For each tile the converged steps are the first ones of the window, at most 1 of them. `neighbours`: an entry is 0 wherever the grid of 16 rows of 4 tiles has no neighbour that way.
All inputs are finite; a program needn't handle non-finite values.
Results may differ from a plain program's by a relative error of at most 0.008.
Values may be sent and summed in bfloat16 or wider, within the bound.
No kernel may reach another device: no remote copies, remote signals or barrier semaphores. Data moves between devices by JAX's collectives and lax.ppermute only.
A program may use at most 128 MiB of HBM per device.

v0:
```python
import jax
import jax.numpy as jnp
from jax import lax
from jax.sharding import PartitionSpec as P

GRID_COLS = 4


def copy_for_each(value, axis):
    copies = jnp.broadcast_to(value, (lax.axis_size(axis), *value.shape))
    return lax.all_to_all(copies, axis, split_axis=0, concat_axis=0, tiled=True)


def laid_out(parts, dim):
    dims = list(parts.shape[1:])
    dims[dim] *= parts.shape[0]
    return jnp.moveaxis(parts, 0, dim).reshape(dims)


def gathered_copies(value, axis, dim):
    parts = copy_for_each(value, axis)
    return laid_out(parts, dim)


def shifted(value, axis, steps):
    count = lax.axis_size(axis)
    first, last = (max(0, -steps), min(count, count - steps))
    return lax.ppermute(value, axis, [(source, source + steps) for source in range(first, last)])


def in_blocks(value, dim, count):
    before, after = (value.shape[:dim], value.shape[dim + 1 :])
    return jnp.moveaxis(value.reshape(*before, count, -1, *after), dim, 0)


def sum_at_owner(value, axis, dim):
    parts = in_blocks(value, dim, lax.axis_size(axis))
    arrived = lax.all_to_all(parts, axis, split_axis=0, concat_axis=0, tiled=True)
    return arrived.astype(jnp.float32).sum(axis=0)


def entering(value, axis, join, neutral):
    place = lax.axis_index(axis)
    gathered = lax.all_gather(value.astype(jnp.bfloat16), axis)
    state = jnp.zeros_like(value) + jnp.asarray(neutral, value.dtype)

    def one(lap, state):
        return join(state, lax.dynamic_index_in_dim(gathered, lap, 0, False).astype(value.dtype))

    return lax.fori_loop(0, place, one, state)


def attend(queries, keys_all, values_all, key_mask, factor):
    scores = (
        jnp.einsum("sqhd,skhd->shqk", queries, keys_all, preferred_element_type=jnp.float32)
        * factor
    )
    expo = jnp.exp(scores) * key_mask
    probs = (expo / jnp.sum(expo, axis=-1, keepdims=True)).astype(jnp.bfloat16)
    attended = jnp.einsum("shqk,skhd->sqhd", probs, values_all, preferred_element_type=jnp.float32)
    return attended.astype(jnp.bfloat16)


def rms_gain(block, gain):
    return (
        block / jnp.sqrt(jnp.mean(block * block, axis=-1, keepdims=True) + 1e-06) * gain
    ).astype(jnp.bfloat16)


def add_terms(earlier, later):
    return earlier + later


def body(
    latents,
    start,
    cached_velocity,
    shift,
    scale,
    gate,
    step_sizes,
    converged,
    neighbours,
    w_qkv,
    q_gain,
    k_gain,
    w_out,
):
    tile_tokens = latents.shape[1]
    width = latents.shape[2]
    group_cols = w_qkv.shape[2]
    head_size = q_gain.shape[0]
    group_heads = group_cols // head_size
    step_count = converged.shape[0]
    own = latents[0]
    mean = jnp.mean(own, axis=-1, keepdims=True)
    var = jnp.mean(jnp.square(own - mean), axis=-1, keepdims=True)
    normed = ((own - mean) / jnp.sqrt(var + 1e-06) * (1.0 + scale) + shift).astype(jnp.bfloat16)[
        None
    ]
    block = gathered_copies(normed, "step", 0)
    count = block.shape[0]
    project_flat = block.reshape(count * tile_tokens, width)
    result = jnp.einsum("rd,cdf->crf", project_flat, w_qkv, preferred_element_type=jnp.float32)
    qkv = result.reshape(3, count, tile_tokens, group_cols)
    qkv = qkv.reshape(3, step_count, tile_tokens, group_heads, head_size)
    queries = rms_gain(qkv[0], q_gain)
    keys_own = rms_gain(qkv[1], k_gain)
    values_own = qkv[2].astype(jnp.bfloat16)
    stacked = jnp.stack([keys_own, values_own]).reshape(2, step_count, tile_tokens, group_cols)
    collected = [stacked]
    for offset in (1, -1, GRID_COLS, -GRID_COLS):
        collected.append(shifted(stacked, "tile", offset))
    joined = jnp.concatenate(collected, axis=2).reshape(
        2, step_count, 5 * tile_tokens, group_heads, head_size
    )
    key_mask = jnp.concatenate(
        [
            jnp.ones((tile_tokens,), jnp.float32),
            jnp.repeat(neighbours[0].astype(jnp.float32), tile_tokens),
        ]
    )
    factor = 1.0 / jnp.sqrt(jnp.float32(head_size))
    results = []
    for position in range(step_count):

        def fresh(_, position=position):
            return attend(
                queries[position : position + 1],
                joined[0, position : position + 1],
                joined[1, position : position + 1],
                key_mask,
                factor,
            )

        def blank(_, position=position):
            return jnp.zeros((1, tile_tokens, group_heads, head_size), jnp.bfloat16)

        results.append(lax.cond(converged[position, 0] > 0, blank, fresh, 0))
    attended = jnp.concatenate(results, axis=0)
    attended = attended.reshape(step_count, tile_tokens, group_cols)
    flat = attended.reshape(step_count * tile_tokens, group_cols)
    terms = jnp.dot(
        flat, lax.all_gather(w_out, "tile", axis=1, tiled=True), preferred_element_type=jnp.float32
    )
    terms = terms.reshape(step_count, tile_tokens, width)
    projected = sum_at_owner(terms.astype(jnp.bfloat16), "step", 0)
    here = lax.axis_index("step")
    flag = lax.dynamic_slice_in_dim(converged, here, 1, 0)[0, 0]
    velocity = jnp.where(flag > 0, cached_velocity, gate[:, None, :] * projected)
    scaled = step_sizes[:, None, None] * velocity
    prefix = entering(scaled, "step", add_terms, jnp.zeros_like(scaled))
    updated = start[None, :, :] + prefix
    return (updated, velocity)


def solution(mesh):
    placed = (
        P("step", "tile", None),
        P("tile", None),
        P("step", "tile", None),
        P("step", None),
        P("step", None),
        P("step", None),
        P("step"),
        P(None, "tile"),
        P("tile", None),
        P(None, None, "step"),
        P(),
        P(),
        P("step", "tile"),
    )
    return jax.shard_map(
        body,
        mesh=mesh,
        in_specs=placed,
        out_specs=(P("step", "tile", None), P("step", "tile", None)),
        check_vma=False,
    )
```

profile of v0, /device:TPU:1, one launch (start us, length us, event | category | flops | bytes accessed | tf_op | source)
XLA Modules:
  0.0 156.8 jit_solution(7559792582649957298)
XLA Ops:
  7.3 0.7 all-gather.4.cloned.1.call-update
  7.9 0.0 all-gather.6.cloned.1.call-start
  8.0 1.6 %reduce_sum.65 = f32[128]{0:T(128)S(1)} reduce(f32[1,128,3072]{2,1,0:T(8,128)} %param.19, f32[]{:T(128)} %constant.42.clone.1), dimensions={0,2}, to_apply=%region_0.0 | reduce | flops 393088 | bytes 1573380 | tf_op jit(solution)/shard_map/reduce_sum | solution.py:96
  9.6 0.3 multiply_reduce_fusion
  9.9 0.3 add_convert_fusion
  10.3 0.2 broadcast_in_dim.10
  10.5 6.0 %all_to_all.10 = bf16[2,1,128,3072]{3,2,1,0:T(8,128)(2,1)S(1)} all-to-all(bf16[2,1,128,3072]{3,2,1,0:T(8,128)(2,1)S(1)} %broadcast_in_dim.10), channel_id=1, replica_groups=mesh['step'=2,'tile'=64] {'step'}, dimensions={0} | all-to-all | bytes 3145728 | tf_op jit(solution)/shard_map/all_to_all | solution.py:11
  16.5 9.0 %convolution_bitcast_fusion = f32[3,256,1024]{2,1,0:T(8,128)S(1)} fusion(bf16[256,3072,1]{1,0,2:T(8,128)(2,1)S(1)} %bitcast.134, bf16[3,3072,1024]{2,1,0:T(8,128)(2,1)} %param.28), kind=kOutput, calls=%fused_computation.30 | convolution fusion | flops 4831838208 | bytes 23592960 | tf_op jit(solution)/shard_map/rd,cdf->crf/dot_general | solution.py:104
  25.5 0.9 slice.76
  26.3 0.3 multiply_bitcast_fusion
  26.6 0.2 copy.48
  26.8 0.3 bitcast_reduce_fusion
  27.2 0.1 copy.38
  27.2 0.3 copy.39
  27.6 1.3 copy.40
  28.9 0.2 fusion.26
  29.2 1.3 pad_maximum_fusion
  30.5 4.2 %collective-permute-start = (bf16[2,2,128,1024]{2,3,1,0:T(8,128)(2,1)S(1)}, bf16[2,2,128,1024]{2,3,1,0:T(8,128)(2,1)}, u32[]{:S(2)}, u32[]{:S(2)}) collective-permute-start(bf16[2,2,128,1024]{2,3,1,0:T(8,128)(2,1)S(1)} %get-tuple-element.101), channel_id=1, source_target_pairs={{0,1},{1,2},{2,3},{3,4},{4,5},{5,6},{6,7},{7,8},{8,9},{9,10},{10,1... | collective-permute-start | bytes 3145736 | tf_op jit(solution)/shard_map/ppermute | solution.py:28
  34.7 1.3 collective-permute-start.1
  36.0 6.3 %collective-permute-start.2 = (bf16[2,2,128,1024]{2,3,1,0:T(8,128)(2,1)S(1)}, bf16[2,2,128,1024]{2,3,1,0:T(8,128)(2,1)}, u32[]{:S(2)}, u32[]{:S(2)}) collective-permute-start(bf16[2,2,128,1024]{2,3,1,0:T(8,128)(2,1)S(1)} %get-tuple-element.101), channel_id=1, source_target_pairs={{0,4},{1,5},{2,6},{3,7},{4,8},{5,9},{6,10},{7,11},{8,12},{9,13},{1... | collective-permute-start | bytes 3145736 | tf_op jit(solution)/shard_map/ppermute | solution.py:28
  42.3 1.3 collective-permute-start.3
  43.6 0.2 copy.47
  43.8 0.3 multiply_reduce_fusion.1
  44.2 0.1 copy.36
  44.2 0.6 constant_dynamic-slice_fusion
  47.4 0.1 broadcast_bitcast_fusion.1
  47.5 0.3 fusion.28
  47.9 10.3 %collective-permute-done = bf16[2,2,128,1024]{2,3,1,0:T(8,128)(2,1)} collective-permute-done((bf16[2,2,128,1024]{2,3,1,0:T(8,128)(2,1)S(1)}, bf16[2,2,128,1024]{2,3,1,0:T(8,128)(2,1)}, u32[]{:S(2)}, u32[]{:S(2)}) %collective-permute-start) | collective-permute-done | bytes 1048608 | tf_op jit(solution)/shard_map/ppermute | solution.py:28
  58.1 2.4 %constant_dynamic-update-slice_fusion.3 = bf16[2,2,640,1024]{2,3,1,0:T(8,128)(2,1)} fusion(bf16[2,2,640,1024]{2,3,1,0:T(8,128)(2,1)} %get-tuple-element.102, bf16[2,2,128,1024]{2,3,1,0:T(8,128)(2,1)} %collective-permute-done), kind=kLoop, calls=%fused_computation.56 | loop fusion | bytes 2097152
  60.5 3.8 %collective-permute-done.1 = bf16[2,2,128,1024]{2,3,1,0:T(8,128)(2,1)} collective-permute-done((bf16[2,2,128,1024]{2,3,1,0:T(8,128)(2,1)S(1)}, bf16[2,2,128,1024]{2,3,1,0:T(8,128)(2,1)}, u32[]{:S(2)}, u32[]{:S(2)}) %collective-permute-start.1) | collective-permute-done | bytes 1048608 | tf_op jit(solution)/shard_map/ppermute | solution.py:28
  64.3 2.4 %constant_dynamic-update-slice_fusion.2 = bf16[2,2,640,1024]{2,3,1,0:T(8,128)(2,1)} fusion(bf16[2,2,640,1024]{2,3,1,0:T(8,128)(2,1)} %constant_dynamic-update-slice_fusion.3, bf16[2,2,128,1024]{2,3,1,0:T(8,128)(2,1)} %collective-permute-done.1), kind=kLoop, calls=%fused_computation.55 | loop fusion | bytes 2097152
  66.7 19.0 %collective-permute-done.2 = bf16[2,2,128,1024]{2,3,1,0:T(8,128)(2,1)} collective-permute-done((bf16[2,2,128,1024]{2,3,1,0:T(8,128)(2,1)S(1)}, bf16[2,2,128,1024]{2,3,1,0:T(8,128)(2,1)}, u32[]{:S(2)}, u32[]{:S(2)}) %collective-permute-start.2) | collective-permute-done | bytes 1048608 | tf_op jit(solution)/shard_map/ppermute | solution.py:28
  85.6 2.3 %constant_dynamic-update-slice_fusion.1 = bf16[2,2,640,1024]{2,3,1,0:T(8,128)(2,1)} fusion(bf16[2,2,640,1024]{2,3,1,0:T(8,128)(2,1)} %constant_dynamic-update-slice_fusion.2, bf16[2,2,128,1024]{2,3,1,0:T(8,128)(2,1)} %collective-permute-done.2), kind=kLoop, calls=%fused_computation.54 | loop fusion | bytes 2097152
  88.0 2.3 %constant_dynamic-update-slice_fusion = bf16[2,2,640,1024]{2,3,1,0:T(8,128)(2,1)} fusion(bf16[2,2,640,1024]{2,3,1,0:T(8,128)(2,1)} %constant_dynamic-update-slice_fusion.1, bf16[2,2,128,1024]{2,3,1,0:T(8,128)(2,1)} %collective-permute-done.3), kind=kLoop, calls=%fused_computation.53 | loop fusion | bytes 2097152 | tf_op jit(solution)/shard_map/concatenate | solution.py:114
  90.3 12.1 %conditional.3 = (bf16[1,128,8,128]{3,1,2,0:T(8,128)(2,1)S(1)}) conditional(s32[]{:T(128)} %bitcast.31, (bf16[2,128,8,128]{3,1,2,0:T(8,128)(2,1)S(1)}, bf16[2,2,640,8,128]{2,4,3,1,0:T(8,128)(2,1)}, f32[640]{0:T(1024)S(1)}) %tuple.67, () %tuple.26), branch_computations={%region_7.0_spmd, %region_9.0_spmd} | conditional | flops 340261888 | bytes 18889224 | solution.py:139
  90.3 7.9 %copy.42 = bf16[2,2,640,8,128]{4,2,3,1,0:T(8,128)(2,1)} copy(bf16[2,2,640,8,128]{2,4,3,1,0:T(8,128)(2,1)} %get-tuple-element.78) | data formatting | bytes 10485760 | tf_op jit(solution)/shard_map
  98.2 2.1 %fusion.8 = (f32[8,128]{1,0:T(8,128)S(1)}, f32[8,128,640]{2,1,0:T(8,128)S(1)}) fusion(f32[640]{0:T(1024)S(1)} %get-tuple-element.39, bf16[2,2,640,8,128]{4,2,3,1,0:T(8,128)(2,1)} %copy.42, bf16[2,128,8,128]{3,1,2,0:T(8,128)(2,1)S(1)} %get-tuple-element.37), kind=kOutput, calls=%fused_computation.14 | convolution fusion | flops 169737216 | bytes 4202496 | tf_op jit(solution)/shard_map/cond/branch_0_fun/sqhd,skhd->shqk/dot_general | solution.py:55
  100.3 2.1 %fusion.12 = bf16[1,128,8,128]{3,1,2,0:T(8,128)(2,1)S(1)} fusion(bf16[2,2,640,8,128]{4,2,3,1,0:T(8,128)(2,1)} %copy.42, f32[8,128,640]{2,1,0:T(8,128)S(1)} %get-tuple-element.97, f32[8,128]{1,0:T(8,128)S(1)} %get-tuple-element.96, f32[640]{0:T(1024)S(1)} %get-tuple-element.39), kind=kOutput, calls=%fused_computation.20 | convolution fusion | flops 170524672 | bytes 4200960 | tf_op jit(solution)/shard_map/cond/branch_0_fun/shqk,skhd->sqhd/dot_general | solution.py:60
  102.4 19.8 %all-gather.4.cloned.1.call-done = bf16[1024,3072]{0,1:T(8,128)(2,1)} async-done(((bf16[1024,48]{0,1:T(8,128)(2,1)}), bf16[1024,3072]{0,1:T(8,128)(2,1)}) %all-gather.4.cloned.1.call-update) | async-done | bytes 6291472 | tf_op jit(solution)/shard_map/all_gather | solution.py:144
  122.2 4.7 %fusion.21 = bf16[2,1,128,3072]{3,2,1,0:T(8,128)(2,1)S(1)} fusion(bf16[1024,3072]{0,1:T(8,128)(2,1)} %all-gather.4.cloned.1.call-done, bf16[1,128,8,128]{3,1,2,0:T(8,128)(2,1)S(1)} %get-tuple-element.154, bf16[1,128,8,128]{3,1,2,0:T(8,128)(2,1)S(1)} %get-tuple-element.153), kind=kOutput, calls=%fused_computation.28 | convolution fusion | flops 1611661312 | bytes 8388608 | tf_op jit(solution)/shard_map/dot_general | solution.py:143
  126.9 5.9 %all_to_all.11 = bf16[2,1,128,3072]{3,2,1,0:T(8,128)(2,1)S(1)} all-to-all(bf16[2,1,128,3072]{3,2,1,0:T(8,128)(2,1)S(1)} %fusion.21), channel_id=1, replica_groups=mesh['step'=2,'tile'=64] {'step'}, dimensions={0} | all-to-all | bytes 3145728 | tf_op jit(solution)/shard_map/all_to_all | solution.py:38
  132.7 0.3 convert_reduce_fusion
  133.1 1.7 %multiply_convert_fusion = (bf16[1,128,3072]{2,1,0:T(8,128)(2,1)}, f32[1,128,3072]{2,1,0:T(8,128)}) fusion(f32[]{:T(128)} %bitcast.128, f32[1,128,3072]{2,1,0:T(8,128)S(1)} %copy-done.4, f32[128,3072]{1,0:T(8,128)S(1)} %convert_reduce_fusion, f32[3072]{0:T(1024)S(1)} %bitcast.140, pred[]{:T(512)} %bitcast.15), kind=kLoop, calls=%fused_computation.35 | loop fusion | flops 1572864 | bytes 5517317 | tf_op jit(solution)/shard_map/convert_element_type | solution.py:44
  134.8 12.1 %all-gather.6.cloned.1.call-done = bf16[2,128,3072]{2,1,0:T(8,128)(2,1)} async-done(((bf16[1,128,3072]{2,1,0:T(8,128)(2,1)}), bf16[2,128,3072]{2,1,0:T(8,128)(2,1)}) %all-gather.6.cloned.1.call-update) | async-done | bytes 1572880 | tf_op jit(solution)/shard_map/all_gather | solution.py:44
  146.8 0.1 broadcast_in_dim.9
  147.0 1.6 %while.10 = (s32[]{:T(128)}, f32[1,128,3072]{2,1,0:T(8,128)S(1)}, s32[]{:T(128)}, bf16[2,1,128,3072]{3,2,1,0:T(8,128)(2,1)}, s32[]{:T(128)}, /*index=5*/s32[]{:T(128)}, s32[]{:T(128)}) while((s32[]{:T(128)}, f32[1,128,3072]{2,1,0:T(8,128)S(1)}, s32[]{:T(128)}, bf16[2,1,128,3072]{3,2,1,0:T(8,128)(2,1)}, s32[]{:T(128)}, ...), condition=%wide.region_12.13_spmd, body=%wide.region_11.12_spmd.sunk | while | flops 786437 | bytes 3932275 | solution.py:50
  147.0 1.6 %convert_add_fusion.2 = f32[1,128,3072]{2,1,0:T(8,128)S(1)} fusion(f32[1,128,3072]{2,1,0:T(8,128)S(1)} %get-tuple-element.140, bf16[2,1,128,3072]{3,2,1,0:T(8,128)(2,1)} %get-tuple-element.149, s32[]{:T(128)S(6)} %select_n.23), kind=kLoop, calls=%fused_computation.24.clone.1 | loop fusion | flops 786432 | bytes 3932164 | tf_op jit(solution)/shard_map/while/body/add | solution.py:71
  148.7 1.3 bitcast_add_fusion
  (35 shorter events, 0.3 us)
Async XLA Ops:
  7.2 21.7 %copy-start = (f32[128]{0:T(128)S(1)}, f32[128]{0:T(128)}, u32[]{:S(2)}) copy-start(f32[128]{0:T(128)} %param.30) | copy-start | bytes 1540
  7.2 2.4 %copy-start.2 = (f32[1,128,3072]{2,1,0:T(8,128)S(1)}, f32[1,128,3072]{2,1,0:T(8,128)}, u32[]{:S(2)}) copy-start(f32[1,128,3072]{2,1,0:T(8,128)} %param.19) | copy-start | bytes 4718596
  7.2 2.7 %copy-start.6 = (f32[1,3072]{1,0:T(1,128)S(1)}, f32[1,3072]{1,0:T(1,128)}, u32[]{:S(2)}) copy-start(f32[1,3072]{1,0:T(1,128)} %param.23) | copy-start | bytes 36868
  7.2 2.7 %copy-start.5 = (f32[1,3072]{1,0:T(1,128)S(1)}, f32[1,3072]{1,0:T(1,128)}, u32[]{:S(2)}) copy-start(f32[1,3072]{1,0:T(1,128)} %param.22) | copy-start | bytes 36868
  7.2 114.9 %all-gather.4.cloned.1.call-start = ((), (), s32[]{:S(2)}) async-start(), calls=%async_computation.2 | async-start | bytes 6389760 | tf_op jit(solution)/shard_map/all_gather | solution.py:144
  7.9 138.9 %all-gather.6.cloned.1.call-start = ((), (), s32[]{:S(2)}) async-start(), calls=%async_computation.3 | async-start | bytes 2359296 | tf_op jit(solution)/shard_map/all_gather | solution.py:44
  28.9 14.7 %copy-start.10 = (s32[1,4]{1,0:T(1,128)S(1)}, s32[1,4]{1,0:T(1,128)}, u32[]{:S(2)}) copy-start(s32[1,4]{1,0:T(1,128)} %param.27) | copy-start | bytes 52
  29.2 15.1 %copy-start.8 = (s32[2,1]{0,1:T(1,128)S(1)}, s32[2,1]{0,1:T(1,128)}, u32[]{:S(2)}) copy-start(s32[2,1]{0,1:T(1,128)} %param.26) | copy-start | bytes 28
  29.2 18.3 %copy-start.9 = (f32[128]{0:T(128)S(1)}, f32[128]{0:T(128)}, u32[]{:S(2)}) copy-start(f32[128]{0:T(128)} %param.29) | copy-start | bytes 1540
  30.5 27.6 %collective-permute-start = (bf16[2,2,128,1024]{2,3,1,0:T(8,128)(2,1)S(1)}, bf16[2,2,128,1024]{2,3,1,0:T(8,128)(2,1)}, u32[]{:S(2)}, u32[]{:S(2)}) collective-permute-start(bf16[2,2,128,1024]{2,3,1,0:T(8,128)(2,1)S(1)} %get-tuple-element.101), channel_id=1, source_target_pairs={{0,1},{1,2},{2,3},{3,4},{4,5},{5,6},{6,7},{7,8},{8,9},{9,10},{10,1... | collective-permute-start | bytes 3145736 | tf_op jit(solution)/shard_map/ppermute | solution.py:28
  34.7 29.6 %collective-permute-start.1 = (bf16[2,2,128,1024]{2,3,1,0:T(8,128)(2,1)S(1)}, bf16[2,2,128,1024]{2,3,1,0:T(8,128)(2,1)}, u32[]{:S(2)}, u32[]{:S(2)}) collective-permute-start(bf16[2,2,128,1024]{2,3,1,0:T(8,128)(2,1)S(1)} %get-tuple-element.101), channel_id=1, source_target_pairs={{1,0},{2,1},{3,2},{4,3},{5,4},{6,5},{7,6},{8,7},{9,8},{10,9},{11,1... | collective-permute-start | bytes 3145736 | tf_op jit(solution)/shard_map/ppermute | solution.py:28
  36.0 49.6 %collective-permute-start.2 = (bf16[2,2,128,1024]{2,3,1,0:T(8,128)(2,1)S(1)}, bf16[2,2,128,1024]{2,3,1,0:T(8,128)(2,1)}, u32[]{:S(2)}, u32[]{:S(2)}) collective-permute-start(bf16[2,2,128,1024]{2,3,1,0:T(8,128)(2,1)S(1)} %get-tuple-element.101), channel_id=1, source_target_pairs={{0,4},{1,5},{2,6},{3,7},{4,8},{5,9},{6,10},{7,11},{8,12},{9,13},{1... | collective-permute-start | bytes 3145736 | tf_op jit(solution)/shard_map/ppermute | solution.py:28
  42.3 45.7 %collective-permute-start.3 = (bf16[2,2,128,1024]{2,3,1,0:T(8,128)(2,1)S(1)}, bf16[2,2,128,1024]{2,3,1,0:T(8,128)(2,1)}, u32[]{:S(2)}, u32[]{:S(2)}) collective-permute-start(bf16[2,2,128,1024]{2,3,1,0:T(8,128)(2,1)S(1)} %get-tuple-element.101), channel_id=1, source_target_pairs={{4,0},{5,1},{6,2},{7,3},{8,4},{9,5},{10,6},{11,7},{12,8},{13,9},{1... | collective-permute-start | bytes 3145736 | tf_op jit(solution)/shard_map/ppermute | solution.py:28
  126.9 6.2 %copy-start.4 = (f32[1,128,3072]{2,1,0:T(8,128)S(1)}, f32[1,128,3072]{2,1,0:T(8,128)}, u32[]{:S(2)}) copy-start(f32[1,128,3072]{2,1,0:T(8,128)} %param.21) | copy-start | bytes 4718596
  126.9 6.2 %copy-start.7 = (f32[1,3072]{1,0:T(1,128)S(1)}, f32[1,3072]{1,0:T(1,128)}, u32[]{:S(2)}) copy-start(f32[1,3072]{1,0:T(1,128)} %param.24) | copy-start | bytes 36868
  147.0 1.7 %copy-start.3 = (f32[128,3072]{1,0:T(8,128)S(1)}, f32[128,3072]{1,0:T(8,128)}, u32[]{:S(2)}) copy-start(f32[128,3072]{1,0:T(8,128)} %param.20) | copy-start | bytes 4718596
  148.7 1.3 copy-start.1
Sparse Core Ops, SparseCore 0:
  10.8 111.3 all-gather.3
  134.9 11.9 all-gather.5
where the time goes:
time: 158 us; the launch traced here: 157 us
  waiting for transfers between devices  65.6 us (42%)
  local copies, waits for them, and re-layouts  21.4 us (14%)
  matrix products  17.9 us (11%)
  between operations  17 us (11%)
  starting transfers between devices  13.1 us (8%)
  blocking collectives  11.9 us (8%)
  other arithmetic  10 us (6%)
    ppermute x4, waiting for transfers between devices, shifted(): lax.ppermute(value, axis, [(source, source + steps) for source in range(f...  33 us
    all_gather x1, waiting for transfers between devices, body(): lax.all_gather(w_out, 'tile', axis=1, tiled=True)  19.8 us
    ppermute x4, starting transfers between devices, shifted(): lax.ppermute(value, axis, [(source, source + steps) for source in range(f...  13 us
    all_gather x1, waiting for transfers between devices, entering(): gathered = lax.all_gather(value.astype(jnp.bfloat16), axis)  12.1 us
    dot_general x1, matrix products, body(): jnp.einsum('rd,cdf->crf', project_flat, w_qkv, preferred_element_type=jnp...  8.97 us
    another operation x2, local copies, waits for them, and re-layouts  7.92 us
    unnamed x27, local copies, waits for them, and re-layouts  7.54 us
    all_to_all x1, blocking collectives, copy_for_each(): return lax.all_to_all(copies, axis, split_axis=0, concat_axis=0, tiled=True)  6.01 us
  transfers between devices with their start and end apart: 6, of which 5 were waited for; matrix products, arithmetic and copies ran while one was open for 25% of the time, Pallas kernels for 0%

commit v1 on v0

--- a/solution.py
+++ b/solution.py
@@ -1,9 +1,23 @@
+import functools
 import jax
 import jax.numpy as jnp
 from jax import lax
 from jax.sharding import PartitionSpec as P
 
 GRID_COLS = 4
+
+
+def _bind_members_all(point, pos_dim):
+    near = jnp.concatenate(
+        lax.all_to_all(
+            jnp.stack([point for _ in range(lax.axis_size("tile"))], axis=0), "tile", 0, 0
+        ),
+        axis=pos_dim,
+    )
+    return near
+
+
+shape_goods = functools.partial(_bind_members_all, pos_dim=1)
 
 
 def copy_for_each(value, axis):
@@ -140,9 +154,7 @@
     attended = jnp.concatenate(results, axis=0)
     attended = attended.reshape(step_count, tile_tokens, group_cols)
     flat = attended.reshape(step_count * tile_tokens, group_cols)
-    terms = jnp.dot(
-        flat, lax.all_gather(w_out, "tile", axis=1, tiled=True), preferred_element_type=jnp.float32
-    )
+    terms = jnp.dot(flat, shape_goods(w_out), preferred_element_type=jnp.float32)
     terms = terms.reshape(step_count, tile_tokens, width)
     projected = sum_at_owner(terms.astype(jnp.bfloat16), "step", 0)
     here = lax.axis_index("step")

time: 158 us -> 220 us (1.39)
  waiting for transfers between devices: 65.6 us -> 113 us
  starting transfers between devices: 13.1 us -> 24 us
  local copies, waits for them, and re-layouts: 21.4 us -> 24.9 us
    ppermute x4, waiting for transfers between devices: 33 us -> 82.8 us  [shifted(): lax.ppermute(value, axis, [(source, source + steps) for source in range(f...]
    all_gather x1 -> x0, waiting for transfers between devices: 19.8 us -> none  [body(): lax.all_gather(w_out, 'tile', axis=1, tiled=True)]
    all_gather x1, waiting for transfers between devices: 12.1 us -> 30 us  [entering(): gathered = lax.all_gather(value.astype(jnp.bfloat16), axis)]
    all_to_all x0 -> x1, starting transfers between devices: none -> 11.5 us  [_bind_members_all(): lax.all_to_all(jnp.stack([point for _ in range(lax.axis_size('tile'))], a...]
    another operation x2 -> x3, local copies, waits for them, and re-layouts: 7.92 us -> 11.3 us
    unnamed x27 -> x29, local copies, waits for them, and re-layouts: 7.54 us -> 7.57 us
  transfers between devices with their start and end apart: 6 -> 6, of which waited for: 5 -> 3; matrix products, arithmetic and copies ran while one was open for 25% -> 17% of each run, Pallas kernels for 0% -> 0%
where the time goes in v1:
time: 220 us; the launch traced here: 219 us
  waiting for transfers between devices  113 us (51%)
  local copies, waits for them, and re-layouts  24.9 us (11%)
  starting transfers between devices  24 us (11%)
  matrix products  17.9 us (8%)
  between operations  17 us (8%)
  blocking collectives  12 us (5%)
  other arithmetic  10.1 us (5%)
    ppermute x4, waiting for transfers between devices, shifted(): lax.ppermute(value, axis, [(source, source + steps) for source in range(f...  82.8 us
    all_gather x1, waiting for transfers between devices, entering(): gathered = lax.all_gather(value.astype(jnp.bfloat16), axis)  30 us
    ppermute x4, starting transfers between devices, shifted(): lax.ppermute(value, axis, [(source, source + steps) for source in range(f...  12.5 us
    all_to_all x1, starting transfers between devices, _bind_members_all(): lax.all_to_all(jnp.stack([point for _ in range(lax.axis_size('tile'))], a...  11.5 us
    dot_general x1, matrix products, body(): jnp.einsum('rd,cdf->crf', project_flat, w_qkv, preferred_element_type=jnp...  9.02 us
    another operation x2, local copies, waits for them, and re-layouts  7.88 us
    unnamed x29, local copies, waits for them, and re-layouts  7.57 us
    all_to_all x1, blocking collectives, copy_for_each(): return lax.all_to_all(copies, axis, split_axis=0, concat_axis=0, tiled=True)  6.01 us
  transfers between devices with their start and end apart: 6, of which 3 were waited for; matrix products, arithmetic and copies ran while one was open for 17% of the time, Pallas kernels for 0%

profile of v1, /device:TPU:1, one launch (start us, length us, event | category | flops | bytes accessed | tf_op | source)
XLA Modules:
  0.0 219.0 jit_solution(17727364482030104567)
XLA Ops:
  7.2 1.7 reduce_sum.65
  8.9 0.2 copy-done.2
  9.1 0.3 multiply_reduce_fusion
  9.4 0.3 add_convert_fusion
  9.8 0.2 broadcast_in_dim.10
  10.0 6.0 %all_to_all.15 = bf16[2,1,128,3072]{3,2,1,0:T(8,128)(2,1)S(1)} all-to-all(bf16[2,1,128,3072]{3,2,1,0:T(8,128)(2,1)S(1)} %broadcast_in_dim.10), channel_id=1, replica_groups=mesh['step'=2,'tile'=64] {'step'}, dimensions={0} | all-to-all | bytes 3145728 | tf_op jit(solution)/shard_map/all_to_all | solution.py:25
  16.0 3.5 %stack.5 = bf16[64,1024,48]{1,2,0:T(8,128)(2,1)} broadcast(bf16[1024,48]{0,1:T(8,128)(2,1)S(1)} %copy-done.5), dimensions={1,2} | broadcast | bytes 6389760 | tf_op jit(solution)/shard_map/stack | solution.py:13
  19.5 11.5 %all-to-all-start.1 = ((bf16[64,1024,48]{1,2,0:T(8,128)(2,1)}), bf16[64,1024,48]{1,2,0:T(8,128)(2,1)}, u32[]{:S(2)}, u32[]{:S(2)}) async-start(bf16[64,1024,48]{1,2,0:T(8,128)(2,1)} %stack.5), calls=%async_computation.1 | async-start | bytes 12582912 | tf_op jit(solution)/shard_map/all_to_all | solution.py:12
  30.9 0.0 all-gather.3.cloned.1.call-start
  31.0 9.0 %convolution_bitcast_fusion = f32[3,256,1024]{2,1,0:T(8,128)S(1)} fusion(bf16[256,3072,1]{1,0,2:T(8,128)(2,1)S(1)} %bitcast.133, bf16[3,3072,1024]{2,1,0:T(8,128)(2,1)} %param.28), kind=kOutput, calls=%fused_computation.28 | convolution fusion | flops 4831838208 | bytes 23592960 | tf_op jit(solution)/shard_map/rd,cdf->crf/dot_general | solution.py:118
  40.0 0.9 slice.76
  40.9 0.3 multiply_bitcast_fusion
  41.2 0.2 copy.54
  41.4 0.3 bitcast_reduce_fusion
  41.7 0.1 copy.41
  41.8 0.3 copy.42
  42.1 1.3 copy.43
  43.5 0.2 fusion.19
  43.8 1.3 pad_maximum_fusion
  45.1 3.8 %collective-permute-start = (bf16[2,2,128,1024]{2,3,1,0:T(8,128)(2,1)S(1)}, bf16[2,2,128,1024]{2,3,1,0:T(8,128)(2,1)}, u32[]{:S(2)}, u32[]{:S(2)}) collective-permute-start(bf16[2,2,128,1024]{2,3,1,0:T(8,128)(2,1)S(1)} %get-tuple-element.101), channel_id=1, source_target_pairs={{0,1},{1,2},{2,3},{3,4},{4,5},{5,6},{6,7},{7,8},{8,9},{9,10},{10,1... | collective-permute-start | bytes 3145736 | tf_op jit(solution)/shard_map/ppermute | solution.py:42
  48.9 1.3 collective-permute-start.1
  50.2 6.1 %collective-permute-start.2 = (bf16[2,2,128,1024]{2,3,1,0:T(8,128)(2,1)S(1)}, bf16[2,2,128,1024]{2,3,1,0:T(8,128)(2,1)}, u32[]{:S(2)}, u32[]{:S(2)}) collective-permute-start(bf16[2,2,128,1024]{2,3,1,0:T(8,128)(2,1)S(1)} %get-tuple-element.101), channel_id=1, source_target_pairs={{0,4},{1,5},{2,6},{3,7},{4,8},{5,9},{6,10},{7,11},{8,12},{9,13},{1... | collective-permute-start | bytes 3145736 | tf_op jit(solution)/shard_map/ppermute | solution.py:42
  56.3 1.3 collective-permute-start.3
  57.6 0.2 copy.53
  57.8 0.3 multiply_reduce_fusion.1
  58.2 0.1 copy.39
  58.2 0.6 constant_dynamic-slice_fusion
  61.5 0.1 broadcast_bitcast_fusion.1
  61.6 0.3 fusion.21
  61.9 75.1 %collective-permute-done = bf16[2,2,128,1024]{2,3,1,0:T(8,128)(2,1)} collective-permute-done((bf16[2,2,128,1024]{2,3,1,0:T(8,128)(2,1)S(1)}, bf16[2,2,128,1024]{2,3,1,0:T(8,128)(2,1)}, u32[]{:S(2)}, u32[]{:S(2)}) %collective-permute-start) | collective-permute-done | bytes 1048608 | tf_op jit(solution)/shard_map/ppermute | solution.py:42
  137.0 2.3 %constant_dynamic-update-slice_fusion.3 = bf16[2,2,640,1024]{2,3,1,0:T(8,128)(2,1)} fusion(bf16[2,2,640,1024]{2,3,1,0:T(8,128)(2,1)} %get-tuple-element.102, bf16[2,2,128,1024]{2,3,1,0:T(8,128)(2,1)} %collective-permute-done), kind=kLoop, calls=%fused_computation.54 | loop fusion | bytes 2097152
  139.3 2.3 %constant_dynamic-update-slice_fusion.2 = bf16[2,2,640,1024]{2,3,1,0:T(8,128)(2,1)} fusion(bf16[2,2,640,1024]{2,3,1,0:T(8,128)(2,1)} %constant_dynamic-update-slice_fusion.3, bf16[2,2,128,1024]{2,3,1,0:T(8,128)(2,1)} %collective-permute-done.1), kind=kLoop, calls=%fused_computation.53 | loop fusion | bytes 2097152
  141.6 7.7 %collective-permute-done.2 = bf16[2,2,128,1024]{2,3,1,0:T(8,128)(2,1)} collective-permute-done((bf16[2,2,128,1024]{2,3,1,0:T(8,128)(2,1)S(1)}, bf16[2,2,128,1024]{2,3,1,0:T(8,128)(2,1)}, u32[]{:S(2)}, u32[]{:S(2)}) %collective-permute-start.2) | collective-permute-done | bytes 1048608 | tf_op jit(solution)/shard_map/ppermute | solution.py:42
  149.3 2.3 %constant_dynamic-update-slice_fusion.1 = bf16[2,2,640,1024]{2,3,1,0:T(8,128)(2,1)} fusion(bf16[2,2,640,1024]{2,3,1,0:T(8,128)(2,1)} %constant_dynamic-update-slice_fusion.2, bf16[2,2,128,1024]{2,3,1,0:T(8,128)(2,1)} %collective-permute-done.2), kind=kLoop, calls=%fused_computation.52 | loop fusion | bytes 2097152
  151.6 2.3 %constant_dynamic-update-slice_fusion = bf16[2,2,640,1024]{2,3,1,0:T(8,128)(2,1)} fusion(bf16[2,2,640,1024]{2,3,1,0:T(8,128)(2,1)} %constant_dynamic-update-slice_fusion.1, bf16[2,2,128,1024]{2,3,1,0:T(8,128)(2,1)} %collective-permute-done.3), kind=kLoop, calls=%fused_computation.51 | loop fusion | bytes 2097152 | tf_op jit(solution)/shard_map/concatenate | solution.py:128
  154.0 12.2 %conditional.3 = (bf16[1,128,8,128]{3,1,2,0:T(8,128)(2,1)S(1)}) conditional(s32[]{:T(128)} %bitcast.31, (bf16[2,128,8,128]{3,1,2,0:T(8,128)(2,1)S(1)}, bf16[2,2,640,8,128]{2,4,3,1,0:T(8,128)(2,1)}, f32[640]{0:T(1024)S(1)}) %tuple.65, () %tuple.26), branch_computations={%region_7.0_spmd, %region_9.0_spmd} | conditional | flops 340261888 | bytes 18889224 | solution.py:153
  154.0 7.8 %copy.45 = bf16[2,2,640,8,128]{4,2,3,1,0:T(8,128)(2,1)} copy(bf16[2,2,640,8,128]{2,4,3,1,0:T(8,128)(2,1)} %get-tuple-element.78) | data formatting | bytes 10485760 | tf_op jit(solution)/shard_map
  161.8 2.1 fusion.8
  163.9 2.1 fusion.12
  166.2 4.7 %fusion.16 = bf16[2,1,128,3072]{3,2,1,0:T(8,128)(2,1)S(1)} fusion(bf16[1024,3072,1]{0,1,2:T(8,128)(2,1)} %bitcast.34, bf16[1,128,8,128]{3,1,2,0:T(8,128)(2,1)S(1)} %get-tuple-element.154, bf16[1,128,8,128]{3,1,2,0:T(8,128)(2,1)S(1)} %get-tuple-element.153), kind=kOutput, calls=%fused_computation.26 | convolution fusion | flops 1611661312 | bytes 8388608 | tf_op jit(solution)/shard_map/dot_general | solution.py:157
  170.9 6.0 %all_to_all.16 = bf16[2,1,128,3072]{3,2,1,0:T(8,128)(2,1)S(1)} all-to-all(bf16[2,1,128,3072]{3,2,1,0:T(8,128)(2,1)S(1)} %fusion.16), channel_id=1, replica_groups=mesh['step'=2,'tile'=64] {'step'}, dimensions={0} | all-to-all | bytes 3145728 | tf_op jit(solution)/shard_map/all_to_all | solution.py:52
  176.9 0.3 convert_reduce_fusion
  177.2 1.7 multiply_convert_fusion
  178.9 30.0 %all-gather.3.cloned.1.call-done = bf16[2,128,3072]{2,1,0:T(8,128)(2,1)} async-done(((bf16[1,128,3072]{2,1,0:T(8,128)(2,1)}), bf16[2,128,3072]{2,1,0:T(8,128)(2,1)}) %all-gather.3.cloned.1.call-update) | async-done | bytes 1572880 | tf_op jit(solution)/shard_map/all_gather | solution.py:58
  209.0 0.1 broadcast_in_dim.9
  209.1 1.6 while.10
  209.2 1.6 convert_add_fusion.2
  210.8 1.3 bitcast_add_fusion
  (37 shorter events, 0.2 us)
Async XLA Ops:
  7.2 36.3 %copy-start = (f32[128]{0:T(128)S(1)}, f32[128]{0:T(128)}, u32[]{:S(2)}) copy-start(f32[128]{0:T(128)} %param.30) | copy-start | bytes 1540
  7.2 1.9 copy-start.2
  7.2 2.2 %copy-start.7 = (f32[1,3072]{1,0:T(1,128)S(1)}, f32[1,3072]{1,0:T(1,128)}, u32[]{:S(2)}) copy-start(f32[1,3072]{1,0:T(1,128)} %param.23) | copy-start | bytes 36868
  7.2 2.2 %copy-start.6 = (f32[1,3072]{1,0:T(1,128)S(1)}, f32[1,3072]{1,0:T(1,128)}, u32[]{:S(2)}) copy-start(f32[1,3072]{1,0:T(1,128)} %param.22) | copy-start | bytes 36868
  9.8 6.2 %copy-start.5 = (bf16[1024,48]{0,1:T(8,128)(2,1)S(1)}, bf16[1024,48]{0,1:T(8,128)(2,1)}, u32[]{:S(2)}) copy-start(bf16[1024,48]{0,1:T(8,128)(2,1)} %param.31) | copy-start | bytes 294916
  19.5 146.7 %all-to-all-start.1 = ((bf16[64,1024,48]{1,2,0:T(8,128)(2,1)}), bf16[64,1024,48]{1,2,0:T(8,128)(2,1)}, u32[]{:S(2)}, u32[]{:S(2)}) async-start(bf16[64,1024,48]{1,2,0:T(8,128)(2,1)} %stack.5), calls=%async_computation.1 | async-start | bytes 12582912 | tf_op jit(solution)/shard_map/all_to_all | solution.py:12
  30.9 178.0 %all-gather.3.cloned.1.call-start = ((), (), s32[]{:S(2)}) async-start(), calls=%async_computation.3 | async-start | bytes 2359296 | tf_op jit(solution)/shard_map/all_gather | solution.py:58
  43.4 14.2 %copy-start.11 = (s32[1,4]{1,0:T(1,128)S(1)}, s32[1,4]{1,0:T(1,128)}, u32[]{:S(2)}) copy-start(s32[1,4]{1,0:T(1,128)} %param.27) | copy-start | bytes 52
  43.7 14.5 %copy-start.9 = (s32[2,1]{0,1:T(1,128)S(1)}, s32[2,1]{0,1:T(1,128)}, u32[]{:S(2)}) copy-start(s32[2,1]{0,1:T(1,128)} %param.26) | copy-start | bytes 28
  43.7 17.8 %copy-start.10 = (f32[128]{0:T(128)S(1)}, f32[128]{0:T(128)}, u32[]{:S(2)}) copy-start(f32[128]{0:T(128)} %param.29) | copy-start | bytes 1540
  45.1 91.9 %collective-permute-start = (bf16[2,2,128,1024]{2,3,1,0:T(8,128)(2,1)S(1)}, bf16[2,2,128,1024]{2,3,1,0:T(8,128)(2,1)}, u32[]{:S(2)}, u32[]{:S(2)}) collective-permute-start(bf16[2,2,128,1024]{2,3,1,0:T(8,128)(2,1)S(1)} %get-tuple-element.101), channel_id=1, source_target_pairs={{0,1},{1,2},{2,3},{3,4},{4,5},{5,6},{6,7},{7,8},{8,9},{9,10},{10,1... | collective-permute-start | bytes 3145736 | tf_op jit(solution)/shard_map/ppermute | solution.py:42
  48.9 90.4 %collective-permute-start.1 = (bf16[2,2,128,1024]{2,3,1,0:T(8,128)(2,1)S(1)}, bf16[2,2,128,1024]{2,3,1,0:T(8,128)(2,1)}, u32[]{:S(2)}, u32[]{:S(2)}) collective-permute-start(bf16[2,2,128,1024]{2,3,1,0:T(8,128)(2,1)S(1)} %get-tuple-element.101), channel_id=1, source_target_pairs={{1,0},{2,1},{3,2},{4,3},{5,4},{6,5},{7,6},{8,7},{9,8},{10,9},{11,1... | collective-permute-start | bytes 3145736 | tf_op jit(solution)/shard_map/ppermute | solution.py:42
  50.2 99.1 %collective-permute-start.2 = (bf16[2,2,128,1024]{2,3,1,0:T(8,128)(2,1)S(1)}, bf16[2,2,128,1024]{2,3,1,0:T(8,128)(2,1)}, u32[]{:S(2)}, u32[]{:S(2)}) collective-permute-start(bf16[2,2,128,1024]{2,3,1,0:T(8,128)(2,1)S(1)} %get-tuple-element.101), channel_id=1, source_target_pairs={{0,4},{1,5},{2,6},{3,7},{4,8},{5,9},{6,10},{7,11},{8,12},{9,13},{1... | collective-permute-start | bytes 3145736 | tf_op jit(solution)/shard_map/ppermute | solution.py:42
  56.3 95.3 %collective-permute-start.3 = (bf16[2,2,128,1024]{2,3,1,0:T(8,128)(2,1)S(1)}, bf16[2,2,128,1024]{2,3,1,0:T(8,128)(2,1)}, u32[]{:S(2)}, u32[]{:S(2)}) collective-permute-start(bf16[2,2,128,1024]{2,3,1,0:T(8,128)(2,1)S(1)} %get-tuple-element.101), channel_id=1, source_target_pairs={{4,0},{5,1},{6,2},{7,3},{8,4},{9,5},{10,6},{11,7},{12,8},{13,9},{1... | collective-permute-start | bytes 3145736 | tf_op jit(solution)/shard_map/ppermute | solution.py:42
  170.9 6.3 %copy-start.4 = (f32[1,128,3072]{2,1,0:T(8,128)S(1)}, f32[1,128,3072]{2,1,0:T(8,128)}, u32[]{:S(2)}) copy-start(f32[1,128,3072]{2,1,0:T(8,128)} %param.21) | copy-start | bytes 4718596
  170.9 6.3 %copy-start.8 = (f32[1,3072]{1,0:T(1,128)S(1)}, f32[1,3072]{1,0:T(1,128)}, u32[]{:S(2)}) copy-start(f32[1,3072]{1,0:T(1,128)} %param.24) | copy-start | bytes 36868
  209.1 1.7 copy-start.3
  210.8 1.3 copy-start.1
Sparse Core Ops, SparseCore 0:
  179.1 29.8 all-gather.2
